TPU v7x, 256 devices: a whole 4x4x8 slice. The times are simulated.
256 devices in a mesh: seq: 16 (over x, y_hi, core), batch: 16 (over y_lo, z).
Axes of the slice: x: 4, y: 4 (y_hi: 2, y_lo: 2; y = y_hi * 2 + y_lo), z: 8, core: 2. Of those that a mesh axis runs over, the one named last changes fastest.
Arguments:
- query_rows: bfloat16 [16, 2048, 2048], P('batch', 'seq'), may hold values from -6 to 6, as said below
- key_rows: bfloat16 [16, 2048, 1024], P('batch', 'seq'), may hold values from -6 to 6, as said below
- value_rows: bfloat16 [16, 2048, 1024], P('batch', 'seq'), may hold values from -6 to 6, as said below
- attn_output: bfloat16 [16, 2048, 2048], P('batch', 'seq'), may hold values from -6 to 6, as said below
- output_grad: bfloat16 [16, 2048, 2048], P('batch', 'seq'), may hold values from -6 to 6
- log_norm: float32 [16, 16, 2048], P('batch', None, 'seq'), as said below
- slab_order: int32 [16, 16], P('batch', 'seq'), may hold values from 0 to 15, as said below
- normed_input: bfloat16 [16, 2048, 4608], P('batch', 'seq'), may hold values from -6 to 6
Outputs:
- grad_query: bfloat16 [16, 2048, 2048], P('batch', 'seq')
- grad_key: bfloat16 [16, 2048, 1024], P('batch', 'seq')
- grad_weight: float32 [4608, 1024], P('seq')
Inputs may be any that keep to these rules, and one draw needn't show every extreme that they name: `query_rows`: queries of a causal forward pass with 16 heads. `key_rows`: keys of the same forward pass with 8 heads. `value_rows`: values of the same forward pass. `attn_output`: the forward pass's output: for each head, sum over keys at or before the query's position of exp(score - log_norm) times the value. `log_norm`: log of the sum of exp(score) over the keys at or before the query's position, so that each row's weights sum to one. `slab_order`: each row is a permutation of the slab places.
All inputs are finite; a program needn't handle non-finite values.
Results may differ from a plain program's by a relative error of at most 0.025.
Values may be sent and summed in bfloat16 or wider, within the bound.
A program may use at most 128 MiB of HBM per device.

v0:
```python
import jax
import jax.numpy as jnp
from jax import lax
from jax.sharding import PartitionSpec as P

HEADS = 16
KV_HEADS = 8
HEAD = 128


SCALE = 144.0 ** (-0.5)


def from_everyone(shard, axis):
    count = lax.axis_size(axis)
    return lax.all_to_all(
        jnp.broadcast_to(shard[None], (count, *shard.shape)), axis, 0, 0, tiled=True
    )


def joined_along(parts, dim):
    parts = jnp.moveaxis(parts, 0, dim)
    shape = parts.shape
    return parts.reshape(*shape[:dim], shape[dim] * shape[dim + 1], *shape[dim + 2 :])


def gathered_copies(shard, axis, dim):
    parts = from_everyone(shard, axis)
    return joined_along(parts, dim)


def in_one_piece(arrays, axis, dim, along):
    widths = [a.shape[along] for a in arrays]
    both = jnp.concatenate(arrays, axis=along)
    filled = lax.all_gather(both, axis, axis=dim, tiled=True)
    return tuple(jnp.split(filled, [sum(widths[:k]) for k in range(1, len(widths))], axis=along))


def in_blocks(shard, dim, count):
    shape = shard.shape
    parts = shard.reshape(*shape[:dim], count, shape[dim] // count, *shape[dim + 1 :])
    return jnp.moveaxis(parts, dim, 0)


def sum_at_owner(shard, axis, dim):
    count = lax.axis_size(axis)
    parts = lax.all_to_all(in_blocks(shard, dim, count), axis, 0, 0, tiled=True)
    return jnp.sum(parts.astype(jnp.float32), axis=0)


def sent_together(arrays, axis, dim, along):
    ends, at = ([], 0)
    for a in arrays[:-1]:
        at += a.shape[along]
        ends.append(at)
    both = jnp.concatenate(arrays, axis=along)
    return tuple(
        jnp.split(lax.psum_scatter(both, axis, scatter_dimension=dim, tiled=True), ends, axis=along)
    )


def block_terms(queries, grads, delta, norms, query_pos, key_block, value_block, key_pos):
    keys_count = key_block.shape[0]
    scores = SCALE * jnp.einsum(
        "tgrd,kgd->grtk", queries, key_block, preferred_element_type=jnp.float32
    )
    allowed = key_pos[None, :] <= query_pos[:, None]
    probs = jnp.where(allowed, jnp.exp(scores - norms[..., None]), 0.0)
    dprob = jnp.einsum("tgrd,kgd->grtk", grads, value_block, preferred_element_type=jnp.float32)
    dscore = probs * (dprob - delta[..., None])
    probs_low = probs.astype(jnp.bfloat16)
    dscore_low = dscore.astype(jnp.bfloat16)
    grad_q = SCALE * jnp.einsum(
        "grtk,kgd->tgrd", dscore_low, key_block, preferred_element_type=jnp.float32
    )
    grad_k = SCALE * jnp.einsum(
        "grtk,tgrd->kgd", dscore_low, queries, preferred_element_type=jnp.float32
    )
    grad_v = jnp.einsum("grtk,tgrd->kgd", probs_low, grads, preferred_element_type=jnp.float32)
    return (grad_q, grad_k.reshape(keys_count, -1), grad_v.reshape(keys_count, -1))


def local(
    query_rows, key_rows, value_rows, attn_output, output_grad, log_norm, slab_order, normed_input
):
    tokens = query_rows.shape[1]
    group = HEADS // KV_HEADS
    kv_width = KV_HEADS * HEAD
    slabs = lax.axis_size("seq")
    length = tokens * slabs
    orders = gathered_copies(slab_order, "seq", 1)
    queries = query_rows[0].reshape(tokens, KV_HEADS, group, HEAD)
    grads = output_grad[0].reshape(tokens, KV_HEADS, group, HEAD)
    outputs = attn_output[0].reshape(tokens, KV_HEADS, group, HEAD)
    delta = jnp.transpose(
        jnp.sum(grads.astype(jnp.float32) * outputs.astype(jnp.float32), axis=3), (1, 2, 0)
    )
    norms = log_norm[0].reshape(KV_HEADS, group, tokens)
    offsets = jnp.arange(tokens, dtype=jnp.int32)
    query_pos = slab_order[0, 0] * tokens + offsets
    width = tokens * -(-512 // tokens)
    empty_kv = jnp.zeros((length, kv_width), jnp.float32)
    empty_q = jnp.zeros((tokens, KV_HEADS, group, HEAD), jnp.float32)
    start = jnp.int32(0)
    grad_q = empty_q
    grad_k = empty_kv
    grad_v = empty_kv
    key_part, value_part = in_one_piece((key_rows, value_rows), "seq", 1, 0)
    count = key_part.shape[1]
    for begin in range(0, count, width):
        finish = min(begin + width, count)
        shards = (finish - begin) // tokens
        first = (start + begin) // tokens
        places = lax.dynamic_slice_in_dim(orders[0], first, shards, 0)
        key_pos = (places[:, None] * tokens + offsets[None, :]).reshape(-1)
        key_block = key_part[0, begin:finish].reshape(-1, KV_HEADS, HEAD)
        value_block = value_part[0, begin:finish].reshape(-1, KV_HEADS, HEAD)
        term_q, term_k, term_v = block_terms(
            queries, grads, delta, norms, query_pos, key_block, value_block, key_pos
        )
        grad_q = grad_q + term_q
        grad_k = lax.dynamic_update_slice_in_dim(grad_k, term_k, begin, 0)
        grad_v = lax.dynamic_update_slice_in_dim(grad_v, term_v, begin, 0)
    grad_q, part_key, part_value = (grad_q, grad_k, grad_v)
    key_sum, value_sum = tuple(
        (
            part.astype(jnp.float32)
            for part in sent_together(
                (part_key.astype(jnp.bfloat16), part_value.astype(jnp.bfloat16)), "seq", 0, 1
            )
        )
    )
    partial_weight = lax.dot_general(
        normed_input[0],
        value_sum.astype(jnp.bfloat16),
        (((0,), (0,)), ((), ())),
        preferred_element_type=jnp.float32,
    )
    columns = lax.psum_scatter(
        partial_weight.astype(jnp.bfloat16), "batch", scatter_dimension=1, tiled=True
    )
    block = sum_at_owner(columns, "seq", 0)
    weight = gathered_copies(block.astype(jnp.bfloat16), "batch", 1).astype(block.dtype)
    grad_query = grad_q.astype(jnp.bfloat16).reshape(1, tokens, HEADS * HEAD)
    grad_key = key_sum.astype(jnp.bfloat16).reshape(1, tokens, kv_width)
    return (grad_query, grad_key, weight)


def solution(mesh):
    placed = (
        P("batch", "seq", None),
        P("batch", "seq", None),
        P("batch", "seq", None),
        P("batch", "seq", None),
        P("batch", "seq", None),
        P("batch", None, "seq"),
        P("batch", "seq"),
        P("batch", "seq", None),
    )
    return jax.shard_map(
        local,
        mesh=mesh,
        in_specs=placed,
        out_specs=(P("batch", "seq", None), P("batch", "seq", None), P("seq", None)),
        check_vma=False,
    )
```

profile of v0, /device:TPU:1, one launch (start us, length us, event | category | flops | bytes accessed | tf_op | source)
XLA Modules:
  0.0 469.2 jit_solution(12361176742124739413)
XLA Ops:
  11.8 8.4 %all-to-all-start = ((s32[16,1,1]{2,1,0:T(1,128)}), s32[16,1,1]{2,1,0:T(1,128)S(1)}, u32[]{:S(2)}, u32[]{:S(2)}) async-start(s32[16,1,1]{2,1,0:T(1,128)} %broadcast_in_dim.27), calls=%async_computation | async-start | bytes 16384 | tf_op jit(solution)/shard_map/all_to_all | solution.py:16
  25.0 2.4 multiply_reduce_fusion
  28.6 71.0 %all-gather.2.cloned.1.call-done = bf16[2,2048,1024]{1,2,0:T(8,128)(2,1)} async-done(((bf16[2,128,1024]{1,2,0:T(8,128)(2,1)}), bf16[2,2048,1024]{1,2,0:T(8,128)(2,1)}) %all-gather.2.cloned.1.call-update) | async-done | bytes 8388624 | tf_op jit(solution)/shard_map/all_gather | solution.py:35
  99.6 5.9 %fusion.61 = (bf16[1,512,1024]{1,2,0:T(8,128)(2,1)}, bf16[1,512,1024]{1,2,0:T(8,128)(2,1)S(1)}, bf16[1,512,1024]{1,2,0:T(8,128)(2,1)}, bf16[1,512,1024]{1,2,0:T(...) fusion(bf16[2,2048,1024]{1,2,0:T(8,128)(2,1)} %all-gather.2.clo, ...), kind=kLoop, calls=%fused_computation.96 | loop fusion | bytes 16777216 | tf_op jit(solution)/shard_map/slice | solution.py:117
  110.2 2.3 copy.196
  112.5 4.0 fusion.2
  119.6 2.3 copy.184
  124.6 2.8 fusion.6
  127.4 2.3 copy.193
  129.6 3.4 bitcast_multiply_fusion.1
  133.0 2.3 copy.181
  139.2 2.8 fusion.10
  142.1 2.3 copy.190
  144.4 3.4 bitcast_multiply_fusion.2
  147.7 2.3 copy.178
  154.0 2.8 fusion.14
  156.8 2.3 copy.187
  159.1 3.4 bitcast_multiply_fusion.3
  162.4 2.4 copy.175
  164.8 3.8 dynamic_update_slice.24
  168.6 2.5 dynamic_update_slice.28
  177.5 8.2 %pad_maximum_fusion = bf16[2048,2048]{1,0:T(8,128)(2,1)} fusion(bf16[2048,1024]{1,0:T(8,128)(2,1)} %constant_dynamic-update-slice_fusion, bf16[2048,1024]{1,0:T(8,128)(2,1)} %constant_dynamic-update-slice_fusion.3), kind=kLoop, calls=%fused_computation.1 | loop fusion | flops 16777216 | bytes 16777216 | tf_op jit(solution)/shard_map/concatenate | solution.py:56
  185.7 106.7 %reduce-scatter.3.cloned.1.call-done = bf16[128,2048]{1,0:T(8,128)(2,1)} async-done(((bf16[2048,2048]{1,0:T(8,128)(2,1)}), bf16[128,2048]{1,0:T(8,128)(2,1)}) %reduce-scatter.3.cloned.1.call-update) | async-done | bytes 524304 | tf_op jit(solution)/shard_map/reduce_scatter | solution.py:58
  292.4 6.1 %fusion = bf16[4608,1024]{0,1:T(8,128)(2,1)} fusion(bf16[1,128,4608]{2,1,0:T(8,128)(2,1)S(1)} %copy-done, bf16[128,2048]{1,0:T(8,128)(2,1)} %reduce-scatter.3.cloned.1.call-done), kind=kOutput, calls=%fused_computation.2 | convolution fusion | flops 1212678144 | bytes 10878976 | tf_op jit(solution)/shard_map/dot_general | solution.py:133
  298.5 112.2 %reduce-scatter.5.cloned.1.call-done = bf16[4608,64]{0,1:T(8,128)(2,1)} async-done(((bf16[4608,1024]{0,1:T(8,128)(2,1)}), bf16[4608,64]{0,1:T(8,128)(2,1)}) %reduce-scatter.5.cloned.1.call-update) | async-done | bytes 589840 | tf_op jit(solution)/shard_map/reduce_scatter | solution.py:139
  410.7 2.2 reshape.164
  414.0 7.3 %all-to-all-start.1 = ((bf16[16,288,64]{1,2,0:T(8,128)(2,1)}), bf16[16,288,64]{1,2,0:T(8,128)(2,1)}, u32[]{:S(2)}, u32[]{:S(2)}) async-start(bf16[16,288,64]{1,2,0:T(8,128)(2,1)} %copy.197), calls=%async_computation.3 | async-start | bytes 1572864 | tf_op jit(solution)/shard_map/all_to_all | solution.py:47
  421.3 3.4 fusion.63
  424.7 10.3 %all-to-all-done.1 = bf16[16,288,64]{1,2,0:T(8,128)(2,1)} async-done(((bf16[16,288,64]{1,2,0:T(8,128)(2,1)}), bf16[16,288,64]{1,2,0:T(8,128)(2,1)}, u32[]{:S(2)}, u32[]{:S(2)}) %all-to-all-start.1) | async-done | bytes 589856 | tf_op jit(solution)/shard_map/all_to_all | solution.py:47
  437.3 4.3 all-to-all-start.2
  441.6 2.5 convolution_add_fusion.2
  447.3 12.6 %all-to-all-done.2 = bf16[16,288,64]{1,2,0:T(8,128)(2,1)} async-done(((bf16[16,288,64]{1,2,0:T(8,128)(2,1)}), bf16[16,288,64]{1,2,0:T(8,128)(2,1)}, u32[]{:S(2)}, u32[]{:S(2)}) %all-to-all-start.2) | async-done | bytes 589856 | tf_op jit(solution)/shard_map/all_to_all | solution.py:16
  (91 shorter events, 43.9 us)
Async XLA Ops:
  7.2 285.3 %copy-start = (bf16[1,128,4608]{2,1,0:T(8,128)(2,1)S(1)}, bf16[1,128,4608]{2,1,0:T(8,128)(2,1)}, u32[]{:S(2)}) copy-start(bf16[1,128,4608]{2,1,0:T(8,128)(2,1)} %param.15) | copy-start | bytes 3538948
  7.2 15.6 %copy-start.20 = (bf16[1,128,2048]{2,1,0:T(8,128)(2,1)S(1)}, bf16[1,128,2048]{2,1,0:T(8,128)(2,1)}, u32[]{:S(2)}) copy-start(bf16[1,128,2048]{2,1,0:T(8,128)(2,1)} %param.8) | copy-start | bytes 1572868
  7.2 15.9 %copy-start.19 = (bf16[1,128,2048]{2,1,0:T(8,128)(2,1)S(1)}, bf16[1,128,2048]{2,1,0:T(8,128)(2,1)}, u32[]{:S(2)}) copy-start(bf16[1,128,2048]{2,1,0:T(8,128)(2,1)} %param.11) | copy-start | bytes 1572868
  7.2 92.4 %all-gather.2.cloned.1.call-start = ((), (), s32[]{:S(2)}) async-start(), calls=%async_computation.5 | async-start | bytes 8912896 | tf_op jit(solution)/shard_map/all_gather | solution.py:35
  11.8 15.9 %all-to-all-start = ((s32[16,1,1]{2,1,0:T(1,128)}), s32[16,1,1]{2,1,0:T(1,128)S(1)}, u32[]{:S(2)}, u32[]{:S(2)}) async-start(s32[16,1,1]{2,1,0:T(1,128)} %broadcast_in_dim.27), calls=%async_computation | async-start | bytes 16384 | tf_op jit(solution)/shard_map/all_to_all | solution.py:16
  20.2 272.2 %reduce-scatter.3.cloned.1.call-start = ((), (), s32[]{:S(2)}) async-start(), calls=%async_computation.6 | async-start | bytes 8912896 | tf_op jit(solution)/shard_map/reduce_scatter | solution.py:58
  105.5 4.7 %copy-start.2 = (bf16[1,512,1024]{1,2,0:T(8,128)(2,1)}, bf16[1,512,1024]{1,2,0:T(8,128)(2,1)S(1)}, u32[]{:S(2)}) copy-start(bf16[1,512,1024]{1,2,0:T(8,128)(2,1)S(1)} %get-tuple-element.20) | copy-start | bytes 3145732
  105.5 2.7 copy-start.21
  105.5 2.7 copy-start.22
  106.3 2.0 copy-start.7
  116.5 1.3 copy-start.4
  122.6 2.0 copy-start.17
  137.3 2.0 copy-start.16
  152.0 2.0 copy-start.15
  162.4 6.2 %copy-start.14 = (bf16[512,1024]{1,0:T(8,128)(2,1)S(1)}, bf16[512,1024]{1,0:T(8,128)(2,1)}, u32[]{:S(2)}) copy-start(bf16[512,1024]{1,0:T(8,128)(2,1)} %copy.187) | copy-start | bytes 3145732
  164.8 6.3 %copy-start.13 = (bf16[512,1024]{1,0:T(8,128)(2,1)S(1)}, bf16[512,1024]{1,0:T(8,128)(2,1)}, u32[]{:S(2)}) copy-start(bf16[512,1024]{1,0:T(8,128)(2,1)} %copy.178) | copy-start | bytes 3145732
  168.6 3.6 copy-start.11
  168.6 4.6 copy-start.9
  171.1 3.1 copy-start.12
  171.1 4.2 copy-start.10
  172.2 4.2 copy-start.8
  185.7 225.0 %reduce-scatter.5.cloned.1.call-start = ((), (), s32[]{:S(2)}) async-start(), calls=%async_computation.7 | async-start | bytes 10027008 | tf_op jit(solution)/shard_map/reduce_scatter | solution.py:139
  414.0 27.5 %copy-start.1 = (bf16[1,512,1024]{1,2,0:T(8,128)(2,1)S(1)}, bf16[1,512,1024]{1,2,0:T(8,128)(2,1)}, u32[]{:S(2)}) copy-start(bf16[1,512,1024]{1,2,0:T(8,128)(2,1)} %get-tuple-element.24) | copy-start | bytes 3145732
  414.0 21.0 %all-to-all-start.1 = ((bf16[16,288,64]{1,2,0:T(8,128)(2,1)}), bf16[16,288,64]{1,2,0:T(8,128)(2,1)}, u32[]{:S(2)}, u32[]{:S(2)}) async-start(bf16[16,288,64]{1,2,0:T(8,128)(2,1)} %copy.197), calls=%async_computation.3 | async-start | bytes 1572864 | tf_op jit(solution)/shard_map/all_to_all | solution.py:47
  437.3 22.7 %all-to-all-start.2 = ((bf16[16,288,64]{1,2,0:T(8,128)(2,1)}), bf16[16,288,64]{1,2,0:T(8,128)(2,1)}, u32[]{:S(2)}, u32[]{:S(2)}) async-start(bf16[16,288,64]{1,2,0:T(8,128)(2,1)} %broadcast_in_dim.58), calls=%async_computation.4 | async-start | bytes 1572864 | tf_op jit(solution)/shard_map/all_to_all | solution.py:16
  441.6 2.6 copy-start.6
  441.6 3.1 copy-start.3
  441.6 3.5 copy-start.5
  445.0 1.6 copy-start.18
Sparse Core Ops, SparseCore 0:
  11.1 88.3 all-gather.1
  185.8 106.6 reduce-scatter.2
  298.6 112.0 reduce-scatter.4
where the time goes:
time: 472 us; the launch traced here: 469 us
  waiting for transfers between devices  313 us (66%)
  local copies, waits for them, and re-layouts  56 us (12%)
  matrix products  50.7 us (11%)
  starting transfers between devices  20.1 us (4%)
  other arithmetic  14.9 us (3%)
  between operations  14.7 us (3%)
    reduce_scatter x1, waiting for transfers between devices, local(): lax.psum_scatter(partial_weight.astype(jnp.bfloat16), 'batch', scatter_di...  112 us
    reduce_scatter x1, waiting for transfers between devices, sent_together(): lax.psum_scatter(both, axis, scatter_dimension=dim, tiled=True)  107 us
    all_gather x1, waiting for transfers between devices, in_one_piece(): filled = lax.all_gather(both, axis, axis=dim, tiled=True)  71 us
    all_to_all x2, starting transfers between devices, from_everyone(): lax.all_to_all(jnp.broadcast_to(shard[None], (count, *shard.shape)), axis...  12.7 us
    all_to_all x2, waiting for transfers between devices, from_everyone(): lax.all_to_all(jnp.broadcast_to(shard[None], (count, *shard.shape)), axis...  12.6 us
    dot_general x4, matrix products, block_terms(): jnp.einsum('tgrd,kgd->grtk', grads, value_block, preferred_element_type=j...  12.4 us
    dot_general x4, matrix products, block_terms(): jnp.einsum('grtk,tgrd->kgd', dscore_low, queries, preferred_element_type=...  11.9 us
    all_to_all x1, waiting for transfers between devices, sum_at_owner(): parts = lax.all_to_all(in_blocks(shard, dim, count), axis, 0, 0, tiled=True)  10.3 us
  transfers between devices with their start and end apart: 6, of which 5 were waited for; matrix products, arithmetic and copies ran while one was open for 4% of the time, Pallas kernels for 0%

commit v1 on v0

v1 whole, which is shorter than its diff:
```python
import functools

import jax
import jax.numpy as jnp
from jax import lax
from jax.experimental import pallas as pl
from jax.experimental.pallas import tpu as pltpu
from jax.sharding import PartitionSpec as P

HEADS = 16
KV_HEADS = 8
HEAD = 128
TOK = 128
D = 4608
XROWS = D // 4
QROWS = D // 16
HALF = QROWS // 2

SCALE = 144.0 ** (-0.5)
LOG2E = 1.4426950408889634

MESH = pl.DeviceIdType.MESH
F32 = jnp.float32
BF16 = jnp.bfloat16

RELS = ((1, 0), (1, 1), (3, 0), (3, 1), (2, 0), (2, 1), (0, 1))
STEPS = (1, 3, 2)


def dot(a, b):
    return lax.dot_general(a, b, (((1,), (0,)), ((), ())), preferred_element_type=F32)


def dot_nt(a, b):
    return lax.dot_general(a, b, (((1,), (1,)), ((), ())), preferred_element_type=F32)


def kernel(
    q_ref, do_ref, o_ref, k_ref, v_ref, ln_ref, slab_ref, n_ref,
    gq_ref, gk_ref, w_ref,
    pos_s, pos_r, aux_s, aux_r, q_r, do_r, kv_r, nt_s, nt_r, kt, dqt, acc, dkv_s, dkv_r,
    dvg, dq_s, dk_s, wy_s, wy_r, wz_s, wz_r, wa_s, wf,
    x_ss, x_rs, x_ls, y_ss, y_rs, n_ss, n_rs, n_ls, p_ss, p_rs, dy_ss, dy_rs, dv_ss, dv_rs,
    g_ss, g_rs, g_ls, wy_ss, wy_rs, wz_ss, wz_rs, wa_ss, wa_rs,
):
    seq = lax.axis_index("seq")
    batch = lax.axis_index("batch")
    x, yh, c = seq // 4, (seq // 2) % 2, seq % 2
    yl, z = batch // 8, batch % 8
    y = 2 * yh + yl

    def device(x_, y_, c_, z_):
        return {"seq": 4 * x_ + 2 * (y_ // 2) + c_, "batch": 8 * (y_ % 2) + z_}

    def along_x(step):
        return (x + step) % 4

    def remote(src, dst, ss, rs, to):
        copy = pltpu.make_async_remote_copy(
            src_ref=src, dst_ref=dst, send_sem=ss, recv_sem=rs,
            device_id=to, device_id_type=MESH,
        )
        copy.start()
        return copy

    def keep(src, dst, sem):
        copy = pltpu.make_async_copy(src, dst, sem)
        copy.start()
        return copy

    g = 2 * x + c
    partner = device(x, (y + 2) % 4, c, z)
    peers = [device(along_x(dx), y, (c + dc) % 2, z) for dx, dc in RELS]
    slots = [2 * along_x(dx) + (c + dc) % 2 for dx, dc in RELS]
    sources = [2 * along_x(4 - dx) + (c + dc) % 2 for dx, dc in RELS]

    pos_s[...] = jnp.full((8, TOK), slab_ref[0, 0] * TOK, jnp.int32).astype(F32)

    barrier = pltpu.get_barrier_semaphore()
    for to in peers:
        pl.semaphore_signal(barrier, inc=1, device_id=to, device_id_type=MESH)
    for step in STEPS:
        to = device(x, (y + step) % 4, c, z)
        pl.semaphore_signal(barrier, inc=1, device_id=to, device_id_type=MESH)
    for dyl in range(2):
        for dc in range(2):
            for dz in range(8):
                if dyl + dc + dz > 0:
                    to = device(x, 2 * yh + (yl + dyl) % 2, (c + dc) % 2, (z + dz) % 8)
                    pl.semaphore_signal(barrier, inc=1, device_id=to, device_id_type=MESH)
    pl.semaphore_wait(barrier, 41)

    sent = []

    def columns(ref, slot, width):
        return ref.at[:, pl.ds(pl.multiple_of(slot * width, width), width)]

    first, own_first = [], [
        keep(columns(k_ref, g, HEAD), kv_r.at[0, 0, g], x_ls.at[0]),
        keep(columns(v_ref, g, HEAD), kv_r.at[0, 1, g], x_ls.at[1]),
        keep(pos_s, pos_r.at[0, g], x_ls.at[2]),
    ]
    for r, to in enumerate(peers):
        first.append([
            remote(columns(k_ref, slots[r], HEAD), kv_r.at[0, 0, g], x_ss.at[0, r], x_rs.at[0, r], to),
            remote(columns(v_ref, slots[r], HEAD), kv_r.at[0, 1, g], x_ss.at[1, r], x_rs.at[1, r], to),
            remote(pos_s, pos_r.at[0, g], x_ss.at[2, r], x_rs.at[2, r], to),
        ])

    def delta_of(h, carry):
        rows = []
        for e in range(2):
            at = pl.ds(pl.multiple_of((2 * h + e) * HEAD, HEAD), HEAD)
            both = do_ref[:, at].astype(F32) * o_ref[:, at].astype(F32)
            rows.append(jnp.sum(both.T, axis=0, keepdims=True))
        norms = ln_ref[pl.ds(2 * h, 2), :] * LOG2E
        aux_s[h] = jnp.concatenate([norms, *rows, jnp.zeros((4, TOK), F32)], axis=0)
        return carry

    lax.fori_loop(0, KV_HEADS, delta_of, 0)

    second, own_second = [], [
        keep(aux_s.at[g], aux_r.at[g], x_ls.at[3]),
        keep(columns(q_ref, g, 2 * HEAD), q_r.at[g], x_ls.at[4]),
        keep(columns(do_ref, g, 2 * HEAD), do_r.at[g], x_ls.at[5]),
    ]
    for r, to in enumerate(peers):
        second.append([
            remote(columns(q_ref, slots[r], 2 * HEAD), q_r.at[g], x_ss.at[4, r], x_rs.at[4, r], to),
            remote(columns(do_ref, slots[r], 2 * HEAD), do_r.at[g], x_ss.at[5, r], x_rs.at[5, r], to),
            remote(aux_s.at[slots[r]], aux_r.at[g], x_ss.at[3, r], x_rs.at[3, r], to),
        ])

    passed = []

    def pass_on(slot, r):
        passed.append(remote(kv_r.at[0, :, slot], kv_r.at[1, :, slot], y_ss.at[0, r], y_rs.at[0, r], partner))
        passed.append(remote(pos_r.at[0, slot], pos_r.at[1, slot], y_ss.at[1, r], y_rs.at[1, r], partner))

    for copy in own_first:
        copy.wait()
    pass_on(g, 7)

    def turn(b, carry):
        at = pl.ds(pl.multiple_of(b * 128, 128), 128)
        nt_s[at, :] = n_ref[:, at].astype(F32).T.astype(BF16)
        return carry

    lax.fori_loop(0, D // 128, turn, 0)

    for r in range(7):
        for copy in first[r]:
            copy.wait_recv()
        pass_on(sources[r], r)

    def x_rows(step):
        return nt_s.at[pl.ds(pl.multiple_of(along_x(step) * XROWS, 128), XROWS), :]

    inputs = [keep(x_rows(0), nt_r.at[g], n_ls)]
    for i, step in enumerate(STEPS):
        inputs.append(
            remote(x_rows(step), nt_r.at[g], n_ss.at[i], n_rs.at[i], device(along_x(step), y, c, z))
        )

    for copy in own_second:
        copy.wait()
    for r in range(7):
        for copy in second[r]:
            copy.wait_recv()
    for copy in passed:
        copy.wait_recv()

    lane = lax.broadcasted_iota(jnp.int32, (1, TOK), 1).astype(F32)
    key_at = lax.broadcasted_iota(jnp.int32, (TOK, TOK), 0).astype(F32)

    def block(half, b, fresh):
        for k in range(4):
            kt[:, 128 * k : 128 * k + 128] = kv_r[half, 0, 4 * b + k].astype(F32).T.astype(BF16)
        acc[half] = jnp.zeros((2, 512, HEAD), F32)

        def step(j, carry):
            queries = jnp.concatenate([q_r[j, :, :HEAD], q_r[j, :, HEAD:]], axis=0)
            grads = jnp.concatenate([do_r[j, :, :HEAD], do_r[j, :, HEAD:]], axis=0)
            aux = aux_r[j]
            norms = jnp.concatenate([aux[0:1], aux[1:2]], axis=1)
            delta = jnp.concatenate([aux[2:3], aux[3:4]], axis=1)
            query_pos = pos_r[0, j][0:1] + lane
            keys = kv_r[half, 0, 4 * b : 4 * b + 4].reshape(512, HEAD)
            values = kv_r[half, 1, 4 * b : 4 * b + 4].reshape(512, HEAD)
            scores = dot_nt(keys, queries)
            dprob = dot_nt(values, grads)
            probs, dscores = [], []
            for k in range(4):
                rows = slice(128 * k, 128 * k + 128)
                ahead = query_pos - pos_r[half, 4 * b + k][0:1]
                allowed = ahead >= key_at
                prob = jnp.exp2(scores[rows] * (SCALE * LOG2E) - norms)
                prob = jnp.concatenate(
                    [jnp.where(allowed, prob[:, :128], 0.0), jnp.where(allowed, prob[:, 128:], 0.0)], axis=1
                )
                probs.append(prob.astype(BF16))
                dscores.append((prob * (dprob[rows] - delta)).astype(BF16))
            prob = jnp.concatenate(probs, axis=0)
            dscore = jnp.concatenate(dscores, axis=0)
            acc[half, 0] += dot(dscore, queries)
            acc[half, 1] += dot(prob, grads)
            term = dot(kt[...], dscore)
            if fresh:
                dqt[j] = term
            else:
                dqt[j] += term
            return carry

        lax.fori_loop(0, 8, step, 0)

    across = []
    for b in range(2):
        block(1, b, b == 0)
        dkv_s[b] = acc[1].astype(BF16)
        across.append(remote(dkv_s.at[b], dkv_r.at[b], dy_ss.at[b], dy_rs.at[b], partner))

    values_out = []
    for b in range(2):
        block(0, b, False)
        if b == 0:
            for copy in inputs:
                if copy is inputs[0]:
                    copy.wait()
                else:
                    copy.wait_recv()
            shared = []
            other = device(x, y, (c + 1) % 2, z)
            for i in range(4):
                j = 2 * along_x(i) + c
                shared.append(remote(nt_r.at[j], nt_r.at[j], p_ss.at[i], p_rs.at[i], other))
        across[b].wait_recv()
        rows = slice(512 * b, 512 * b + 512)
        dvg[0, rows] = (acc[0, 1] + dkv_r[b, 1].astype(F32)).astype(BF16)
        for i, step in enumerate(STEPS):
            values_out.append(
                remote(
                    dvg.at[0, rows], dvg.at[i + 1, rows], dv_ss.at[b, i], dv_rs.at[b, i],
                    device(along_x(step), y, c, z),
                )
            )
        keys_done = (SCALE * (acc[0, 0] + dkv_r[b, 0].astype(F32))).astype(BF16)
        dk_s[4 * b : 4 * b + 4] = keys_done.reshape(4, 128, HEAD)

    def queries_done(j, carry):
        dq_s[j] = jnp.concatenate(
            [(SCALE * dqt[j, :, :128]).T, (SCALE * dqt[j, :, 128:]).T], axis=1
        ).astype(BF16)
        return carry

    lax.fori_loop(0, 8, queries_done, 0)

    back = [
        keep(dk_s.at[g], columns(gk_ref, g, HEAD), g_ls.at[0]),
        keep(dq_s.at[g], columns(gq_ref, g, 2 * HEAD), g_ls.at[1]),
    ]
    for r, to in enumerate(peers):
        back.append(remote(dk_s.at[slots[r]], columns(gk_ref, g, HEAD), g_ss.at[0, r], g_rs.at[0, r], to))
        back.append(remote(dq_s.at[slots[r]], columns(gq_ref, g, 2 * HEAD), g_ss.at[1, r], g_rs.at[1, r], to))

    for copy in shared:
        copy.wait_recv()

    over_y = []

    def multiply(i):
        if i > 0:
            values_out[i - 1].wait_recv()
            values_out[i + 2].wait_recv()

        def quarter(t, carry):
            at = pl.ds(pl.multiple_of(t * QROWS, 32), QROWS)
            total = None
            for j in range(4):
                left = jnp.concatenate([nt_r[2 * j, at, :], nt_r[2 * j + 1, at, :]], axis=1)
                term = dot(left, dvg[i, 256 * j : 256 * j + 256])
                total = term if total is None else total + term
            wy_s[i, t] = total.astype(BF16)
            return carry

        lax.fori_loop(0, 4, quarter, 0)
        over_y.append([
            remote(
                wy_s.at[i, (y + step) % 4], wy_r.at[i, k], wy_ss.at[i, k], wy_rs.at[i, k],
                device(x, (y + step) % 4, c, z),
            )
            for k, step in enumerate(STEPS)
        ])

    def z_copy(i, r):
        return pltpu.make_async_remote_copy(
            src_ref=wz_s.at[i, r], dst_ref=wz_r.at[z], send_sem=wz_ss.at[i, r], recv_sem=wz_rs.at[z],
            device_id=device(x, y, c, 2 * i + r), device_id_type=MESH,
        )

    def reduce_y(i):
        total = wy_s[i, y].astype(F32)
        for k in range(3):
            over_y[i][k].wait_recv()
            total = total + wy_r[i, k].astype(F32)
        wz_s[i] = total.astype(BF16).reshape(2, HALF, HEAD)
        for r in range(2):
            pl.when(z != 2 * i + r)(lambda: z_copy(i, r).start())

    def w_copy(i, t):
        dyl, dz = t // 8, t % 8
        r = z % 2
        block = 2 * along_x((0, 3, 1, 2)[i]) + c
        return pltpu.make_async_remote_copy(
            src_ref=wa_s, dst_ref=wf.at[block, r], send_sem=wa_ss.at[t], recv_sem=wa_rs.at[block, r],
            device_id=device(x, 2 * yh + (yl + dyl) % 2, yl, (z + dz) % 8), device_id_type=MESH,
        )

    def w_keep(i):
        r = z % 2
        block = 2 * along_x((0, 3, 1, 2)[i]) + c
        return pltpu.make_async_copy(wa_s, wf.at[block, r], wa_rs.at[block, r])

    def reduce_z(i):
        @pl.when(z // 2 == i)
        def _():
            total = wz_s[i, z % 2].astype(F32)
            for k in range(1, 8):
                source = (z + k) % 8
                pltpu.make_async_remote_copy(
                    src_ref=wz_s.at[i, 0], dst_ref=wz_r.at[source], send_sem=wz_ss.at[i, 0],
                    recv_sem=wz_rs.at[source], device_id=device(x, y, c, source), device_id_type=MESH,
                ).wait_recv()
                total = total + wz_r[source].astype(F32)
            wa_s[...] = total.astype(BF16)
            for t in range(1, 16):
                w_copy(i, t).start()
            pl.when(c != yl)(lambda: w_copy(i, 0).start())
            pl.when(c == yl)(lambda: w_keep(i).start())

    multiply(0)
    multiply(1)
    reduce_y(0)
    multiply(2)
    reduce_y(1)
    reduce_z(0)
    multiply(3)
    reduce_y(2)
    reduce_z(1)
    reduce_y(3)
    reduce_z(2)
    reduce_z(3)

    for copy in back:
        if copy is back[0] or copy is back[1]:
            copy.wait()
        else:
            copy.wait_recv()

    for block in range(KV_HEADS):
        for r in range(2):
            pltpu.make_async_copy(wa_s, wf.at[block, r], wa_rs.at[block, r]).wait()
            w_ref[HALF * r : HALF * r + HALF, 128 * block : 128 * block + 128] = wf[block, r].astype(F32)

    for group in first + second + over_y:
        for copy in group:
            copy.wait_send()
    for copy in passed + inputs[1:] + shared + across + values_out + back[2:]:
        copy.wait_send()
    for i in range(4):
        for r in range(2):
            pl.when(z != 2 * i + r)(lambda: z_copy(i, r).wait_send())

        @pl.when(z // 2 == i)
        def _():
            for t in range(1, 16):
                w_copy(i, t).wait_send()
            pl.when(c != yl)(lambda: w_copy(i, 0).wait_send())


def local(
    query_rows, key_rows, value_rows, attn_output, output_grad, log_norm, slab_order, normed_input
):
    vmem = pl.BlockSpec(memory_space=pltpu.VMEM)
    smem = pl.BlockSpec(memory_space=pltpu.SMEM)
    dma = pltpu.SemaphoreType.DMA
    grad_query, grad_key, weight = pl.pallas_call(
        kernel,
        name="step",
        out_shape=(
            jax.ShapeDtypeStruct((TOK, HEADS * HEAD), BF16),
            jax.ShapeDtypeStruct((TOK, KV_HEADS * HEAD), BF16),
            jax.ShapeDtypeStruct((QROWS, KV_HEADS * HEAD), F32),
        ),
        in_specs=[vmem] * 6 + [smem, vmem],
        out_specs=(vmem, vmem, vmem),
        scratch_shapes=[
            pltpu.VMEM((8, TOK), F32),
            pltpu.VMEM((2, 8, 8, TOK), F32),
            pltpu.VMEM((8, 8, TOK), F32),
            pltpu.VMEM((8, 8, TOK), F32),
            pltpu.VMEM((8, TOK, 2 * HEAD), BF16),
            pltpu.VMEM((8, TOK, 2 * HEAD), BF16),
            pltpu.VMEM((2, 2, 8, TOK, HEAD), BF16),
            pltpu.VMEM((D, TOK), BF16),
            pltpu.VMEM((8, XROWS, TOK), BF16),
            pltpu.VMEM((HEAD, 512), BF16),
            pltpu.VMEM((8, HEAD, 2 * TOK), F32),
            pltpu.VMEM((2, 2, 512, HEAD), F32),
            pltpu.VMEM((2, 2, 512, HEAD), BF16),
            pltpu.VMEM((2, 2, 512, HEAD), BF16),
            pltpu.VMEM((4, 1024, HEAD), BF16),
            pltpu.VMEM((8, TOK, 2 * HEAD), BF16),
            pltpu.VMEM((8, TOK, HEAD), BF16),
            pltpu.VMEM((4, 4, QROWS, HEAD), BF16),
            pltpu.VMEM((4, 3, QROWS, HEAD), BF16),
            pltpu.VMEM((4, 2, HALF, HEAD), BF16),
            pltpu.VMEM((8, HALF, HEAD), BF16),
            pltpu.VMEM((HALF, HEAD), BF16),
            pltpu.VMEM((8, 2, HALF, HEAD), BF16),
            dma((6, 7)), dma((6, 7)), dma((6,)),
            dma((2, 8)), dma((2, 8)),
            dma((3,)), dma((3,)), dma,
            dma((4,)), dma((4,)),
            dma((2,)), dma((2,)),
            dma((2, 3)), dma((2, 3)),
            dma((2, 7)), dma((2, 7)), dma((2,)),
            dma((4, 3)), dma((4, 3)),
            dma((4, 2)), dma((8,)),
            dma((16,)), dma((8, 2)),
        ],
        compiler_params=pltpu.CompilerParams(
            collective_id=0, has_side_effects=True, vmem_limit_bytes=50 * 2**20
        ),
    )(
        query_rows[0], output_grad[0], attn_output[0], key_rows[0], value_rows[0],
        log_norm[0], slab_order, normed_input[0],
    )
    return grad_query[None], grad_key[None], weight


def solution(mesh):
    placed = (
        P("batch", "seq", None),
        P("batch", "seq", None),
        P("batch", "seq", None),
        P("batch", "seq", None),
        P("batch", "seq", None),
        P("batch", None, "seq"),
        P("batch", "seq"),
        P("batch", "seq", None),
    )
    return jax.shard_map(
        local,
        mesh=mesh,
        in_specs=placed,
        out_specs=(P("batch", "seq", None), P("batch", "seq", None), P("seq", None)),
        check_vma=False,
    )
```

time: 472 us -> 118 us (0.25)
  waiting for transfers between devices: 313 us -> 0 us
  Pallas kernels: 0 us -> 108 us
  matrix products: 50.7 us -> 0 us
  local copies, waits for them, and re-layouts: 56 us -> 8.22 us
  starting transfers between devices: 20.1 us -> 0 us
  other arithmetic: 14.9 us -> 0 us
  between operations: 14.7 us -> 1.3 us
    reduce_scatter x2 -> x0, waiting for transfers between devices: 219 us -> none  [the longest x1 112 us: local(): lax.psum_scatter(partial_weight.astype(jnp.bfloat16), 'batch', scatter_di...]
    pallas_call x0 -> x1, Pallas kernels: none -> 108 us  [local(): pl.pallas_call(kernel, name='step', out_shape=(jax.ShapeDtypeStruct((TOK,...]
    all_gather x1 -> x0, waiting for transfers between devices: 71 us -> none  [in_one_piece(): filled = lax.all_gather(both, axis, axis=dim, tiled=True)]
    dot_general x21 -> x0, matrix products: 50.7 us -> none  [the longest x4 12.4 us: block_terms(): jnp.einsum('tgrd,kgd->grtk', grads, value_block, preferred_element_type=j...]
    all_to_all x3 -> x0, waiting for transfers between devices: 22.9 us -> none  [the longest x2 12.6 us: from_everyone(): lax.all_to_all(jnp.broadcast_to(shard[None], (count, *shard.shape)), axis...]
    reshape x11 -> x0, local copies, waits for them, and re-layouts: 22.3 us -> none  [the longest x4 9.18 us: block_terms(): grad_k.reshape(keys_count, -1)]
    all_to_all x3 -> x0, starting transfers between devices: 20 us -> none  [the longest x2 12.7 us: from_everyone(): lax.all_to_all(jnp.broadcast_to(shard[None], (count, *shard.shape)), axis...]
    dynamic_update_slice x8 -> x0, local copies, waits for them, and re-layouts: 12.6 us -> none  [the longest x4 6.92 us: local(): grad_k = lax.dynamic_update_slice_in_dim(grad_k, term_k, begin, 0)]
  transfers between devices with their start and end apart: 6 -> 0, of which waited for: 5 -> 0; matrix products, arithmetic and copies ran while one was open for 4% -> 0% of each run, Pallas kernels for 0% -> 0%
where the time goes in v1:
time: 118 us
  Pallas kernels  108 us (92%)
  local copies, waits for them, and re-layouts  8.22 us (7%)
  between operations  1.3 us (1%)
    pallas_call x1, Pallas kernels, local(): pl.pallas_call(kernel, name='step', out_shape=(jax.ShapeDtypeStruct((TOK,...  108 us
    unnamed x15, local copies, waits for them, and re-layouts  8.22 us

profile of v1, /device:TPU:1, one launch (start us, length us, event | category | flops | bytes accessed | tf_op | source)
XLA Modules:
  0.0 117.7 jit_solution(10428410362375531852)
XLA Ops:
  1.3 0.0 copy-start
  1.3 1.0 copy-done
  2.3 0.0 copy-start.1
  2.3 1.0 copy-done.1
  3.4 0.0 copy-start.2
  3.4 1.0 copy-done.2
  4.4 0.0 copy-start.3
  4.4 0.9 copy-done.3
  5.4 0.0 copy-start.4
  5.4 0.9 copy-done.4
  6.3 0.0 copy-start.5
  6.3 0.7 copy-done.5
  7.0 108.2 %step.1 = (bf16[128,2048]{1,0:T(8,128)(2,1)S(1)}, bf16[128,1024]{1,0:T(8,128)(2,1)S(1)}, f32[288,1024]{1,0:T(8,128)S(1)}) custom-call(bf16[128,2048]{1,0:T(8,128)(2,1)S(1)} %bitcast.10, bf16[128,2048]{1,0:T(8,128)(2,1)S(1)} %bitcast.11, bf16[128,2048]{1,0:T(8,128)(2,1)S(1)} %bitcast.12, bf16[128,1024]{1,0:T(8,128)(2,1)S(1)} %bitcast.14, ...), custom_call_target="tpu_custom_call" | custom-call | tf_op jit(solution)/shard_map/step/pallas_call | solution.py:386
  115.2 0.8 copy.15
  116.0 0.7 copy.16
  116.7 1.0 copy.17
Async XLA Ops:
  1.3 1.0 copy-start
  2.3 1.0 copy-start.1
  3.4 1.0 copy-start.2
  4.4 0.9 copy-start.3
  5.4 0.9 copy-start.4
  6.3 0.7 copy-start.5

commit v2 on v1

v2 whole, which is shorter than its diff:
```python
import functools

import jax
import jax.numpy as jnp
from jax import lax
from jax.experimental import pallas as pl
from jax.experimental.pallas import tpu as pltpu
from jax.sharding import PartitionSpec as P

HEADS = 16
KV_HEADS = 8
HEAD = 128
TOK = 128
D = 4608
XROWS = D // 4
QROWS = D // 16
PIECE = QROWS // 8

SCALE = 144.0 ** (-0.5)
LOG2E = 1.4426950408889634

MESH = pl.DeviceIdType.MESH
F32 = jnp.float32
BF16 = jnp.bfloat16

RELS = ((0, 1), (1, 0), (1, 1), (3, 0), (3, 1), (2, 0), (2, 1))
STEPS = (1, 3, 2)


def dot(a, b):
    return lax.dot_general(a, b, (((1,), (0,)), ((), ())), preferred_element_type=F32)


def dot_nt(a, b):
    return lax.dot_general(a, b, (((1,), (1,)), ((), ())), preferred_element_type=F32)


def kernel(
    q_hbm, do_hbm, o_hbm, k_hbm, v_hbm, ln_hbm, n_hbm, slab_ref,
    gq_ref, gk_ref, w_ref,
    q_ref, do_ref, o_ref, k_ref, v_ref, ln_ref, n_ref, in_s, pos_s, pos_r, aux_s, aux_r, q_r, do_r, kv_r, nt_s, nt_r, kt, dqt, acc, dkv_s, dkv_r,
    dvg, dq_s, dk_s, wy_s, wy_r, wz_s, wz_r, mid, wa_s, wf,
    x_ss, x_rs, x_ls, y_ss, y_rs, n_ss, n_rs, n_ls, p_ss, p_rs, dy_ss, dy_rs, dv_ss, dv_rs,
    g_ss, g_rs, g_ls, wy_ss, wy_rs, wz_ss, wz_rs, wm_ss, wm_rs, wo_ss, wo_rs, wa_ss, wa_rs,
):
    seq = lax.axis_index("seq")
    batch = lax.axis_index("batch")
    x, yh, c = seq // 4, (seq // 2) % 2, seq % 2
    yl, z = batch // 8, batch % 8
    y = 2 * yh + yl

    def device(x_, y_, c_, z_):
        return {"seq": 4 * x_ + 2 * (y_ // 2) + c_, "batch": 8 * (y_ % 2) + z_}

    def along_x(step):
        return (x + step) % 4

    def remote(src, dst, ss, rs, to):
        copy = pltpu.make_async_remote_copy(
            src_ref=src, dst_ref=dst, send_sem=ss, recv_sem=rs,
            device_id=to, device_id_type=MESH,
        )
        copy.start()
        return copy

    def keep(src, dst, sem):
        copy = pltpu.make_async_copy(src, dst, sem)
        copy.start()
        return copy

    g = 2 * x + c
    partner = device(x, (y + 2) % 4, c, z)
    peers = [device(along_x(dx), y, (c + dc) % 2, z) for dx, dc in RELS]
    slots = [2 * along_x(dx) + (c + dc) % 2 for dx, dc in RELS]
    sources = [2 * along_x(4 - dx) + (c + dc) % 2 for dx, dc in RELS]

    staged = [
        keep(source, target, in_s.at[i])
        for i, (source, target) in enumerate((
            (k_hbm, k_ref), (v_hbm, v_ref), (do_hbm, do_ref), (o_hbm, o_ref),
            (ln_hbm, ln_ref), (q_hbm, q_ref), (n_hbm, n_ref),
        ))
    ]
    pos_s[...] = jnp.full((8, TOK), slab_ref[0, 0] * TOK, jnp.int32).astype(F32)

    barrier = pltpu.get_barrier_semaphore()
    for to in peers:
        pl.semaphore_signal(barrier, inc=1, device_id=to, device_id_type=MESH)
    for step in STEPS:
        to = device(x, (y + step) % 4, c, z)
        pl.semaphore_signal(barrier, inc=1, device_id=to, device_id_type=MESH)
    for dyl in range(2):
        for dc in range(2):
            for dz in range(8):
                if dyl + dc + dz > 0:
                    to = device(x, 2 * yh + (yl + dyl) % 2, (c + dc) % 2, (z + dz) % 8)
                    pl.semaphore_signal(barrier, inc=1, device_id=to, device_id_type=MESH)
    pl.semaphore_wait(barrier, 41)

    staged[0].wait()
    staged[1].wait()

    def columns(ref, slot, width):
        return ref.at[:, pl.ds(pl.multiple_of(slot * width, width), width)]

    first, own_first = [], [
        keep(columns(k_ref, g, HEAD), kv_r.at[0, 0, g], x_ls.at[0]),
        keep(columns(v_ref, g, HEAD), kv_r.at[0, 1, g], x_ls.at[1]),
        keep(pos_s, pos_r.at[0, g], x_ls.at[2]),
    ]
    for r, to in enumerate(peers):
        first.append([
            remote(columns(k_ref, slots[r], HEAD), kv_r.at[0, 0, g], x_ss.at[0, r], x_rs.at[0, r], to),
            remote(columns(v_ref, slots[r], HEAD), kv_r.at[0, 1, g], x_ss.at[1, r], x_rs.at[1, r], to),
            remote(pos_s, pos_r.at[0, g], x_ss.at[2, r], x_rs.at[2, r], to),
        ])

    for copy in staged[2:6]:
        copy.wait()
    lane = lax.broadcasted_iota(jnp.int32, (1, TOK), 1).astype(F32)
    here = pos_s[0:1, :] + lane

    def delta_of(h, carry):
        rows = []
        for e in range(2):
            at = pl.ds(pl.multiple_of((2 * h + e) * HEAD, HEAD), HEAD)
            both = do_ref[:, at].astype(F32) * o_ref[:, at].astype(F32)
            rows.append(jnp.sum(both.T, axis=0, keepdims=True))
        norms = ln_ref[pl.ds(2 * h, 2), :] * LOG2E
        aux_s[h] = jnp.concatenate([norms, *rows, here, jnp.zeros((3, TOK), F32)], axis=0)
        return carry

    lax.fori_loop(0, KV_HEADS, delta_of, 0)

    second, own_second = [], [
        keep(aux_s.at[g], aux_r.at[0], x_ls.at[3]),
        keep(columns(q_ref, g, 2 * HEAD), q_r.at[0], x_ls.at[4]),
        keep(columns(do_ref, g, 2 * HEAD), do_r.at[0], x_ls.at[5]),
    ]
    for r, to in enumerate(peers):
        second.append([
            remote(columns(q_ref, slots[r], 2 * HEAD), q_r.at[r + 1], x_ss.at[4, r], x_rs.at[4, r], to),
            remote(columns(do_ref, slots[r], 2 * HEAD), do_r.at[r + 1], x_ss.at[5, r], x_rs.at[5, r], to),
            remote(aux_s.at[slots[r]], aux_r.at[r + 1], x_ss.at[3, r], x_rs.at[3, r], to),
        ])

    passed = []

    def pass_on(slot, r):
        passed.append(remote(kv_r.at[0, :, slot], kv_r.at[1, :, slot], y_ss.at[0, r], y_rs.at[0, r], partner))
        passed.append(remote(pos_r.at[0, slot], pos_r.at[1, slot], y_ss.at[1, r], y_rs.at[1, r], partner))

    for copy in own_first:
        copy.wait()
    pass_on(g, 7)

    staged[6].wait()

    def turn(b, carry):
        at = pl.ds(pl.multiple_of(b * 128, 128), 128)
        nt_s[at, :] = n_ref[:, at].astype(F32).T.astype(BF16)
        return carry

    lax.fori_loop(0, D // 128, turn, 0)

    for r in range(7):
        for copy in first[r]:
            copy.wait_recv()
        pass_on(sources[r], r)

    def x_rows(step):
        return nt_s.at[pl.ds(pl.multiple_of(along_x(step) * XROWS, 128), XROWS), :]

    inputs = [keep(x_rows(0), nt_r.at[g], n_ls)]
    for i, step in enumerate(STEPS):
        inputs.append(
            remote(x_rows(step), nt_r.at[g], n_ss.at[i], n_rs.at[i], device(along_x(step), y, c, z))
        )

    key_at = lax.broadcasted_iota(jnp.int32, (TOK, TOK), 0).astype(F32)

    def start(half, b):
        for k in range(4):
            kt[half, b, :, 128 * k : 128 * k + 128] = kv_r[half, 0, 4 * b + k].astype(F32).T.astype(BF16)
        acc[half, b] = jnp.zeros((2, 512, HEAD), F32)

    def block(half, b, low, high, fresh=False):
        def step(j, carry):
            queries = jnp.concatenate([q_r[j, :, :HEAD], q_r[j, :, HEAD:]], axis=0)
            grads = jnp.concatenate([do_r[j, :, :HEAD], do_r[j, :, HEAD:]], axis=0)
            aux = aux_r[j]
            norms = jnp.concatenate([aux[0:1], aux[1:2]], axis=1)
            delta = jnp.concatenate([aux[2:3], aux[3:4]], axis=1)
            query_pos = aux[4:5]
            keys = kv_r[half, 0, 4 * b : 4 * b + 4].reshape(512, HEAD)
            values = kv_r[half, 1, 4 * b : 4 * b + 4].reshape(512, HEAD)
            scores = dot_nt(keys, queries)
            dprob = dot_nt(values, grads)
            probs, dscores = [], []
            for k in range(4):
                rows = slice(128 * k, 128 * k + 128)
                ahead = query_pos - pos_r[half, 4 * b + k][0:1]
                allowed = ahead >= key_at
                prob = jnp.exp2(scores[rows] * (SCALE * LOG2E) - norms)
                prob = jnp.concatenate(
                    [jnp.where(allowed, prob[:, :128], 0.0), jnp.where(allowed, prob[:, 128:], 0.0)], axis=1
                )
                probs.append(prob.astype(BF16))
                dscores.append((prob * (dprob[rows] - delta)).astype(BF16))
            prob = jnp.concatenate(probs, axis=0)
            dscore = jnp.concatenate(dscores, axis=0)
            acc[half, b, 0] += dot(dscore, queries)
            acc[half, b, 1] += dot(prob, grads)
            term = dot(kt[half, b], dscore)
            if fresh:
                dqt[j] = term
            else:
                dqt[j] += term
            return carry

        lax.fori_loop(low, high, step, 0, unroll=2)

    across = {}

    def send_across(b, part):
        dkv_s[b, part] = acc[1, b, part].astype(BF16)
        across[b, part] = remote(
            dkv_s.at[b, part], dkv_r.at[b, part], dy_ss.at[b, part], dy_rs.at[b, part], partner
        )

    values_out = {}

    def finish_values(b):
        across[b, 1].wait_recv()
        dvg[0, 512 * b : 512 * b + 512] = (acc[0, b, 1] + dkv_r[b, 1].astype(F32)).astype(BF16)

    def send_values(b, i):
        rows = slice(512 * b, 512 * b + 512)
        values_out[b, i] = remote(
            dvg.at[0, rows], dvg.at[i + 1, rows], dv_ss.at[b, i], dv_rs.at[b, i],
            device(along_x(STEPS[i]), y, c, z),
        )

    def finish_keys(b):
        across[b, 0].wait_recv()
        keys_done = (SCALE * (acc[0, b, 0] + dkv_r[b, 0].astype(F32))).astype(BF16)
        dk_s[4 * b : 4 * b + 4] = keys_done.reshape(4, 128, HEAD)

    other = device(x, y, (c + 1) % 2, z)
    shared = []

    def share(i, step):
        if i == 0:
            inputs[0].wait()
        else:
            inputs[i].wait_recv()
        j = 2 * along_x(step) + c
        shared.append(remote(nt_r.at[j], nt_r.at[j], p_ss.at[i], p_rs.at[i], other))

    def arrived(low, high):
        for r in range(low, high):
            for copy in second[r]:
                copy.wait_recv()

    start(0, 0)
    for copy in own_second:
        copy.wait()
    arrived(0, 5)
    block(0, 0, 0, 6, fresh=True)
    for copy in passed:
        copy.wait_recv()
    start(1, 0)
    block(1, 0, 0, 6)
    arrived(5, 7)
    block(1, 0, 6, 8, fresh=True)
    send_across(0, 1)
    start(1, 1)
    block(1, 1, 0, 8)
    send_across(1, 1)
    send_across(0, 0)
    send_across(1, 0)
    share(0, 0)
    block(0, 0, 6, 8)
    finish_values(0)
    send_values(0, 0)
    send_values(0, 1)
    start(0, 1)
    block(0, 1, 0, 8)
    finish_values(1)
    send_values(1, 0)
    send_values(1, 1)
    send_values(0, 2)
    send_values(1, 2)
    share(1, 3)
    share(2, 1)
    share(3, 2)

    def queries_done(j, carry):
        dq_s[j] = jnp.concatenate(
            [(SCALE * dqt[j, :, :128]).T, (SCALE * dqt[j, :, 128:]).T], axis=1
        ).astype(BF16)
        return carry

    lax.fori_loop(0, 8, queries_done, 0)

    for copy in shared:
        copy.wait_recv()

    back = []

    def send_back():
        finish_keys(0)
        finish_keys(1)
        back.extend([
            keep(dk_s.at[g], columns(gk_ref, g, HEAD), g_ls.at[0]),
            keep(dq_s.at[0], columns(gq_ref, g, 2 * HEAD), g_ls.at[1]),
        ])
        for r, (dx, dc) in enumerate(RELS):
            to = device(along_x(4 - dx), y, (c + dc) % 2, z)
            back.append(remote(dk_s.at[sources[r]], columns(gk_ref, g, HEAD), g_ss.at[0, r], g_rs.at[0, r], to))
            back.append(remote(dq_s.at[r + 1], columns(gq_ref, g, 2 * HEAD), g_ss.at[1, r], g_rs.at[1, r], to))

    over_y = []

    def multiply(i):
        if i > 0:
            values_out[0, i - 1].wait_recv()
            values_out[1, i - 1].wait_recv()

        def quarter(t, carry):
            at = pl.ds(pl.multiple_of(t * QROWS, 32), QROWS)
            total = None
            for j in range(4):
                left = jnp.concatenate([nt_r[2 * j, at, :], nt_r[2 * j + 1, at, :]], axis=1)
                term = dot(left, dvg[i, 256 * j : 256 * j + 256])
                total = term if total is None else total + term
            wy_s[i, t] = total.astype(BF16)
            return carry

        lax.fori_loop(0, 4, quarter, 0)
        over_y.append([
            remote(
                wy_s.at[i, (y + step) % 4], wy_r.at[i, k], wy_ss.at[i, k], wy_rs.at[i, k],
                device(x, (y + step) % 4, c, z),
            )
            for k, step in enumerate(STEPS)
        ])

    over_z = []

    def reduce_y(i):
        total = wy_s[i, y].astype(F32)
        for k in range(3):
            over_y[i][k].wait_recv()
            total = total + wy_r[i, k].astype(F32)
        for k in range(8):
            wz_s[i, k] = total[PIECE * k : PIECE * k + PIECE].astype(BF16)
        over_z.append([
            remote(
                wz_s.at[i, (z + k) % 8], wz_r.at[i, k - 1], wz_ss.at[i, k - 1], wz_rs.at[i, k - 1],
                device(x, y, c, (z + k) % 8),
            )
            for k in (4, 3, 5, 2, 6, 1, 7)
        ])

    def column_block(i, core):
        return 2 * along_x((0, 3, 1, 2)[i]) + core

    def sum_z(i):
        total = wz_s[i, z].astype(F32)
        for copy in over_z[i]:
            copy.wait_recv()
        for k in range(7):
            total = total + wz_r[i, k].astype(F32)
        return total.astype(BF16)

    def w_copy(t):
        dyl, dz = t // 8, t % 8
        return pltpu.make_async_remote_copy(
            src_ref=wa_s, dst_ref=wf.at[column_block(3, c), z], send_sem=wa_ss.at[t], recv_sem=wa_rs.at[c, z],
            device_id=device(x, 2 * yh + (yl + dyl) % 2, yl, (z + dz) % 8), device_id_type=MESH,
        )

    def last_z():
        wa_s[...] = sum_z(3)
        for t in (12, 4, 11, 3, 13, 5, 10, 2, 14, 6, 9, 1, 15, 7, 8):
            w_copy(t).start()
        pl.when(c != yl)(lambda: w_copy(0).start())
        pl.when(c == yl)(
            lambda: pltpu.make_async_copy(wa_s, wf.at[column_block(3, c), z], wa_rs.at[c, z]).start()
        )

    gathered = []

    def reduce_z(i):
        mid[i, z] = sum_z(i)
        gathered.append([
            remote(
                mid.at[i, z], mid.at[i, z], wm_ss.at[i, k - 1], wm_rs.at[i, k - 1],
                device(x, y, c, (z + k) % 8),
            )
            for k in (4, 3, 5, 2, 6, 1, 7)
        ])

    def near_copy(i):
        block = column_block(i, c)
        return pltpu.make_async_remote_copy(
            src_ref=mid.at[i], dst_ref=wf.at[block], send_sem=wo_ss.at[i, 0], recv_sem=wo_rs.at[block],
            device_id=device(x, y, yl, z), device_id_type=MESH,
        )

    handed = []

    def hand_over(i):
        for copy in gathered[i]:
            copy.wait_recv()
        block = column_block(i, c)
        handed.append(
            remote(
                mid.at[i], wf.at[block], wo_ss.at[i, 1], wo_rs.at[block],
                device(x, 2 * yh + (yl + 1) % 2, yl, z),
            )
        )
        pl.when(c != yl)(lambda: near_copy(i).start())
        pl.when(c == yl)(lambda: pltpu.make_async_copy(mid.at[i], wf.at[block], wo_rs.at[block]).start())

    multiply(0)
    send_back()
    multiply(1)
    multiply(2)
    reduce_y(0)
    multiply(3)
    reduce_y(1)
    reduce_z(0)
    reduce_y(2)
    reduce_z(1)
    hand_over(0)
    reduce_y(3)
    reduce_z(2)
    hand_over(1)
    last_z()
    hand_over(2)

    for copy in back:
        if copy is back[0] or copy is back[1]:
            copy.wait()
        else:
            copy.wait_recv()

    for i in range(4):
        for core in range(2):
            block = column_block(i, core)
            at = pl.ds(pl.multiple_of(128 * block, 128), 128)
            if i < 3:
                pltpu.make_async_copy(mid.at[i], wf.at[block], wo_rs.at[block]).wait()
            for k in range(8):
                if i == 3:
                    pltpu.make_async_copy(wa_s, wf.at[block, k], wa_rs.at[core, k]).wait()
                w_ref[PIECE * k : PIECE * k + PIECE, at] = wf[block, k].astype(F32)

    for group in first + second + over_y + over_z + gathered:
        for copy in group:
            copy.wait_send()
    for copy in passed + inputs[1:] + shared + [*across.values(), *values_out.values()] + back[2:] + handed:
        copy.wait_send()
    for t in range(1, 16):
        w_copy(t).wait_send()
    pl.when(c != yl)(lambda: w_copy(0).wait_send())
    for i in range(3):
        pl.when(c != yl)(lambda: near_copy(i).wait_send())


def local(
    query_rows, key_rows, value_rows, attn_output, output_grad, log_norm, slab_order, normed_input
):
    vmem = pl.BlockSpec(memory_space=pltpu.VMEM)
    smem = pl.BlockSpec(memory_space=pltpu.SMEM)
    dma = pltpu.SemaphoreType.DMA
    grad_query, grad_key, weight = pl.pallas_call(
        kernel,
        name="step",
        out_shape=(
            jax.ShapeDtypeStruct((TOK, HEADS * HEAD), BF16),
            jax.ShapeDtypeStruct((TOK, KV_HEADS * HEAD), BF16),
            jax.ShapeDtypeStruct((QROWS, KV_HEADS * HEAD), F32),
        ),
        in_specs=[pl.BlockSpec(memory_space=pltpu.HBM)] * 7 + [smem],
        out_specs=(vmem, vmem, vmem),
        scratch_shapes=[
            pltpu.VMEM((TOK, HEADS * HEAD), BF16),
            pltpu.VMEM((TOK, HEADS * HEAD), BF16),
            pltpu.VMEM((TOK, HEADS * HEAD), BF16),
            pltpu.VMEM((TOK, KV_HEADS * HEAD), BF16),
            pltpu.VMEM((TOK, KV_HEADS * HEAD), BF16),
            pltpu.VMEM((HEADS, TOK), F32),
            pltpu.VMEM((TOK, D), BF16),
            dma((7,)),
            pltpu.VMEM((8, TOK), F32),
            pltpu.VMEM((2, 8, 8, TOK), F32),
            pltpu.VMEM((8, 8, TOK), F32),
            pltpu.VMEM((8, 8, TOK), F32),
            pltpu.VMEM((8, TOK, 2 * HEAD), BF16),
            pltpu.VMEM((8, TOK, 2 * HEAD), BF16),
            pltpu.VMEM((2, 2, 8, TOK, HEAD), BF16),
            pltpu.VMEM((D, TOK), BF16),
            pltpu.VMEM((8, XROWS, TOK), BF16),
            pltpu.VMEM((2, 2, HEAD, 512), BF16),
            pltpu.VMEM((8, HEAD, 2 * TOK), F32),
            pltpu.VMEM((2, 2, 2, 512, HEAD), F32),
            pltpu.VMEM((2, 2, 512, HEAD), BF16),
            pltpu.VMEM((2, 2, 512, HEAD), BF16),
            pltpu.VMEM((4, 1024, HEAD), BF16),
            pltpu.VMEM((8, TOK, 2 * HEAD), BF16),
            pltpu.VMEM((8, TOK, HEAD), BF16),
            pltpu.VMEM((4, 4, QROWS, HEAD), BF16),
            pltpu.VMEM((4, 3, QROWS, HEAD), BF16),
            pltpu.VMEM((4, 8, PIECE, HEAD), BF16),
            pltpu.VMEM((4, 7, PIECE, HEAD), BF16),
            pltpu.VMEM((3, 8, PIECE, HEAD), BF16),
            pltpu.VMEM((PIECE, HEAD), BF16),
            pltpu.VMEM((8, 8, PIECE, HEAD), BF16),
            dma((6, 7)), dma((6, 7)), dma((6,)),
            dma((2, 8)), dma((2, 8)),
            dma((3,)), dma((3,)), dma,
            dma((4,)), dma((4,)),
            dma((2, 2)), dma((2, 2)),
            dma((2, 3)), dma((2, 3)),
            dma((2, 7)), dma((2, 7)), dma((2,)),
            dma((4, 3)), dma((4, 3)),
            dma((4, 7)), dma((4, 7)),
            dma((3, 7)), dma((3, 7)), dma((3, 2)), dma((8,)),
            dma((16,)), dma((2, 8)),
        ],
        compiler_params=pltpu.CompilerParams(
            collective_id=0, has_side_effects=True, vmem_limit_bytes=44 * 2**20
        ),
    )(
        *(
            pltpu.with_memory_space_constraint(part[0], pltpu.HBM)
            for part in (query_rows, output_grad, attn_output, key_rows, value_rows, log_norm, normed_input)
        ),
        slab_order,
    )
    return grad_query[None], grad_key[None], weight


def solution(mesh):
    placed = (
        P("batch", "seq", None),
        P("batch", "seq", None),
        P("batch", "seq", None),
        P("batch", "seq", None),
        P("batch", "seq", None),
        P("batch", None, "seq"),
        P("batch", "seq"),
        P("batch", "seq", None),
    )
    return jax.shard_map(
        local,
        mesh=mesh,
        in_specs=placed,
        out_specs=(P("batch", "seq", None), P("batch", "seq", None), P("seq", None)),
        check_vma=False,
    )
```

time: 118 us -> 84.3 us (0.71)
  Pallas kernels: 108 us -> 80.4 us
  local copies, waits for them, and re-layouts: 8.22 us -> 2.51 us
    pallas_call x1, Pallas kernels: 108 us -> 80.4 us  [local(): pl.pallas_call(kernel, name='step', out_shape=(jax.ShapeDtypeStruct((TOK,...]
    unnamed x15 -> x3, local copies, waits for them, and re-layouts: 8.22 us -> 2.51 us
where the time goes in v2:
time: 84.3 us; the launch traced here: 84.2 us
  Pallas kernels  80.4 us (95%)
  local copies, waits for them, and re-layouts  2.51 us (3%)
  between operations  1.29 us (2%)
    pallas_call x1, Pallas kernels, local(): pl.pallas_call(kernel, name='step', out_shape=(jax.ShapeDtypeStruct((TOK,...  80.4 us
    unnamed x3, local copies, waits for them, and re-layouts  2.51 us

profile of v2, /device:TPU:1, one launch (start us, length us, event | category | flops | bytes accessed | tf_op | source)
XLA Modules:
  0.0 84.2 jit_solution(3010361775827160528)
XLA Ops:
  1.3 80.4 %step.1 = (bf16[128,2048]{1,0:T(8,128)(2,1)S(1)}, bf16[128,1024]{1,0:T(8,128)(2,1)S(1)}, f32[288,1024]{1,0:T(8,128)S(1)}) custom-call(bf16[128,2048]{1,0:T(8,128)(2,1)} %bitcast.12, bf16[128,2048]{1,0:T(8,128)(2,1)} %bitcast.13, bf16[128,2048]{1,0:T(8,128)(2,1)} %bitcast.14, bf16[128,1024]{1,0:T(8,128)(2,1)} %bitcast.15, bf16[128,1024]{1,0:T(8,128)(2,1)} %bitcast.16, ...), custom_call_target="tpu_custom_call" | custom-call | tf_op jit(solution)/shard_map/step/pallas_call | solution.py:479
  81.7 0.8 copy.15
  82.5 0.7 copy.16
  83.2 1.0 %copy.17 = f32[288,1024]{1,0:T(8,128)} copy(f32[288,1024]{1,0:T(8,128)S(1)} %get-tuple-element.14) | data formatting | bytes 2359296

commit v3 on v2

--- a/solution.py
+++ b/solution.py
@@ -154,6 +154,11 @@
         copy.wait()
     pass_on(g, 7)
 
+    for r in range(7):
+        for copy in first[r]:
+            copy.wait_recv()
+        pass_on(sources[r], r)
+
     staged[6].wait()
 
     def turn(b, carry):
@@ -162,11 +167,6 @@
         return carry
 
     lax.fori_loop(0, D // 128, turn, 0)
-
-    for r in range(7):
-        for copy in first[r]:
-            copy.wait_recv()
-        pass_on(sources[r], r)
 
     def x_rows(step):
         return nt_s.at[pl.ds(pl.multiple_of(along_x(step) * XROWS, 128), XROWS), :]
@@ -327,7 +327,7 @@
             values_out[0, i - 1].wait_recv()
             values_out[1, i - 1].wait_recv()
 
-        def quarter(t, carry):
+        def quarter(t):
             at = pl.ds(pl.multiple_of(t * QROWS, 32), QROWS)
             total = None
             for j in range(4):
@@ -335,16 +335,15 @@
                 term = dot(left, dvg[i, 256 * j : 256 * j + 256])
                 total = term if total is None else total + term
             wy_s[i, t] = total.astype(BF16)
-            return carry
-
-        lax.fori_loop(0, 4, quarter, 0)
-        over_y.append([
-            remote(
-                wy_s.at[i, (y + step) % 4], wy_r.at[i, k], wy_ss.at[i, k], wy_rs.at[i, k],
-                device(x, (y + step) % 4, c, z),
+
+        over_y.append([])
+        for k, step in enumerate((2, 1, 3)):
+            t = (y + step) % 4
+            quarter(t)
+            over_y[i].append(
+                remote(wy_s.at[i, t], wy_r.at[i, k], wy_ss.at[i, k], wy_rs.at[i, k], device(x, t, c, z))
             )
-            for k, step in enumerate(STEPS)
-        ])
+        quarter(y)
 
     over_z = []
 
@@ -425,20 +424,20 @@
         pl.when(c == yl)(lambda: pltpu.make_async_copy(mid.at[i], wf.at[block], wo_rs.at[block]).start())
 
     multiply(0)
-    send_back()
     multiply(1)
     multiply(2)
     reduce_y(0)
     multiply(3)
+    send_back()
     reduce_y(1)
     reduce_z(0)
     reduce_y(2)
+    reduce_y(3)
     reduce_z(1)
     hand_over(0)
-    reduce_y(3)
     reduce_z(2)
+    last_z()
     hand_over(1)
-    last_z()
     hand_over(2)
 
     for copy in back:
@@ -470,20 +469,32 @@
         pl.when(c != yl)(lambda: near_copy(i).wait_send())
 
 
+def write(gq_ref, gk_ref, w_ref, gq_hbm, gk_hbm, w_hbm, sems):
+    copies = [
+        pltpu.make_async_copy(source, target, sems.at[i])
+        for i, (source, target) in enumerate(((w_ref, w_hbm), (gq_ref, gq_hbm), (gk_ref, gk_hbm)))
+    ]
+    for copy in copies:
+        copy.start()
+    for copy in copies:
+        copy.wait()
+
+
 def local(
     query_rows, key_rows, value_rows, attn_output, output_grad, log_norm, slab_order, normed_input
 ):
     vmem = pl.BlockSpec(memory_space=pltpu.VMEM)
     smem = pl.BlockSpec(memory_space=pltpu.SMEM)
     dma = pltpu.SemaphoreType.DMA
-    grad_query, grad_key, weight = pl.pallas_call(
+    shapes = (
+        jax.ShapeDtypeStruct((TOK, HEADS * HEAD), BF16),
+        jax.ShapeDtypeStruct((TOK, KV_HEADS * HEAD), BF16),
+        jax.ShapeDtypeStruct((QROWS, KV_HEADS * HEAD), F32),
+    )
+    results = pl.pallas_call(
         kernel,
         name="step",
-        out_shape=(
-            jax.ShapeDtypeStruct((TOK, HEADS * HEAD), BF16),
-            jax.ShapeDtypeStruct((TOK, KV_HEADS * HEAD), BF16),
-            jax.ShapeDtypeStruct((QROWS, KV_HEADS * HEAD), F32),
-        ),
+        out_shape=shapes,
         in_specs=[pl.BlockSpec(memory_space=pltpu.HBM)] * 7 + [smem],
         out_specs=(vmem, vmem, vmem),
         scratch_shapes=[
@@ -541,6 +552,15 @@
         ),
         slab_order,
     )
+    grad_query, grad_key, weight = pl.pallas_call(
+        write,
+        name="write",
+        out_shape=shapes,
+        in_specs=[vmem] * 3,
+        out_specs=[pl.BlockSpec(memory_space=pltpu.HBM)] * 3,
+        scratch_shapes=[dma((3,))],
+        compiler_params=pltpu.CompilerParams(vmem_limit_bytes=2**20),
+    )(*results)
     return grad_query[None], grad_key[None], weight
 
 

time: 84.3 us -> 81.5 us (0.967)
  local copies, waits for them, and re-layouts: 2.51 us -> 0 us
    unnamed x3 -> x0, local copies, waits for them, and re-layouts: 2.51 us -> none
    pallas_call x1 -> x2, Pallas kernels: 80.4 us -> 80.1 us  [the longest x1 78.8 us: local(): pl.pallas_call(kernel, name='step', out_shape=shapes, in_specs=[pl.BlockS...]
where the time goes in v3:
time: 81.5 us; the launch traced here: 81.4 us
  Pallas kernels  80.1 us (98%)
  between operations  1.29 us (2%)
    pallas_call x1, Pallas kernels, local(): pl.pallas_call(kernel, name='step', out_shape=shapes, in_specs=[pl.BlockS...  78.8 us

profile of v3, /device:TPU:1, one launch (start us, length us, event | category | flops | bytes accessed | tf_op | source)
XLA Modules:
  0.0 81.4 jit_solution(8633480865491201684)
XLA Ops:
  1.3 78.8 %step.1 = (bf16[128,2048]{1,0:T(8,128)(2,1)S(1)}, bf16[128,1024]{1,0:T(8,128)(2,1)S(1)}, f32[288,1024]{1,0:T(8,128)S(1)}) custom-call(bf16[128,2048]{1,0:T(8,128)(2,1)} %bitcast.10, bf16[128,2048]{1,0:T(8,128)(2,1)} %bitcast.11, bf16[128,2048]{1,0:T(8,128)(2,1)} %bitcast.12, bf16[128,1024]{1,0:T(8,128)(2,1)} %bitcast.13, bf16[128,1024]{1,0:T(8,128)(2,1)} %bitcast.14, ...), custom_call_target="tpu_custom_call" | custom-call | tf_op jit(solution)/shard_map/step/pallas_call | solution.py:494
  80.1 1.3 %write.1 = (bf16[128,2048]{1,0:T(8,128)(2,1)}, bf16[128,1024]{1,0:T(8,128)(2,1)}, f32[288,1024]{1,0:T(8,128)}) custom-call(bf16[128,2048]{1,0:T(8,128)(2,1)S(1)} %get-tuple-element.9.gq_ref, bf16[128,1024]{1,0:T(8,128)(2,1)S(1)} %get-tuple-element.10.gk_ref, f32[288,1024]{1,0:T(8,128)S(1)} %get-tuple-element.11.w_ref), custom_call_target="tpu_custom_call" | custom-call | tf_op jit(solution)/shard_map/write/pallas_call | solution.py:555

commit v4 on v3

--- a/solution.py
+++ b/solution.py
@@ -218,7 +218,7 @@
                 dqt[j] += term
             return carry
 
-        lax.fori_loop(low, high, step, 0, unroll=2)
+        lax.fori_loop(low, high, step, 0, unroll=2 if high - low != 8 else 4)
 
     across = {}
 
@@ -337,7 +337,7 @@
             wy_s[i, t] = total.astype(BF16)
 
         over_y.append([])
-        for k, step in enumerate((2, 1, 3)):
+        for k, step in enumerate((1, 3, 2)):
             t = (y + step) % 4
             quarter(t)
             over_y[i].append(
@@ -432,10 +432,10 @@
     reduce_y(1)
     reduce_z(0)
     reduce_y(2)
+    reduce_z(1)
     reduce_y(3)
-    reduce_z(1)
+    reduce_z(2)
     hand_over(0)
-    reduce_z(2)
     last_z()
     hand_over(1)
     hand_over(2)

time: 81.5 us -> 81.2 us (level)
  no operation moved by 1% of the time
where the time goes in v4:
time: 81.2 us; the launch traced here: 81.1 us
  Pallas kernels  79.8 us (98%)
  between operations  1.29 us (2%)
    pallas_call x1, Pallas kernels, local(): pl.pallas_call(kernel, name='step', out_shape=shapes, in_specs=[pl.BlockS...  78.5 us

profile of v4, /device:TPU:1, one launch (start us, length us, event | category | flops | bytes accessed | tf_op | source)
XLA Modules:
  0.0 81.1 jit_solution(6253052121870420454)
XLA Ops:
  1.3 78.5 %step.1 = (bf16[128,2048]{1,0:T(8,128)(2,1)S(1)}, bf16[128,1024]{1,0:T(8,128)(2,1)S(1)}, f32[288,1024]{1,0:T(8,128)S(1)}) custom-call(bf16[128,2048]{1,0:T(8,128)(2,1)} %bitcast.10, bf16[128,2048]{1,0:T(8,128)(2,1)} %bitcast.11, bf16[128,2048]{1,0:T(8,128)(2,1)} %bitcast.12, bf16[128,1024]{1,0:T(8,128)(2,1)} %bitcast.13, bf16[128,1024]{1,0:T(8,128)(2,1)} %bitcast.14, ...), custom_call_target="tpu_custom_call" | custom-call | tf_op jit(solution)/shard_map/step/pallas_call | solution.py:494
  79.8 1.3 %write.1 = (bf16[128,2048]{1,0:T(8,128)(2,1)}, bf16[128,1024]{1,0:T(8,128)(2,1)}, f32[288,1024]{1,0:T(8,128)}) custom-call(bf16[128,2048]{1,0:T(8,128)(2,1)S(1)} %get-tuple-element.9.gq_ref, bf16[128,1024]{1,0:T(8,128)(2,1)S(1)} %get-tuple-element.10.gk_ref, f32[288,1024]{1,0:T(8,128)S(1)} %get-tuple-element.11.w_ref), custom_call_target="tpu_custom_call" | custom-call | tf_op jit(solution)/shard_map/write/pallas_call | solution.py:555
